TPU v7x, 32 devices: a whole 2x2x4 slice. The times are simulated.
32 devices in a mesh: ent: 2 (over x), blk: 4 (over y, core), rel: 4 (over z).
Axes of the slice: x: 2, y: 2, z: 4, core: 2. Of those that a mesh axis runs over, the one named last changes fastest.
Arguments:
- factors: bfloat16 [8192, 256], P(('ent', 'blk')), may hold values from -12 to 12
- heads: int32 [8, 4, 1, 8192], P(None, 'rel', None, ('ent', 'blk')), may hold values from 0 to 1023, as said below
- tails: int32 [8, 4, 1, 8192], P(None, 'rel', None, ('ent', 'blk')), may hold values from 0 to 1023, as said below
- values: float32 [8, 4, 1, 8192], P(None, 'rel', None, ('ent', 'blk')), may hold values from 0.3 to 9
Outputs:
- relation_fit: float32 [32, 256, 256], P(('ent', 'blk', 'rel'))
- residual: float32 [32, 256, 256], P(('ent', 'blk', 'rel'))
Inputs may be any that keep to these rules, and one draw needn't show every extreme that they name: In every aligned tile of 128 triple columns (columns 128 t to 128 t + 127 of one relation) all heads lie in one aligned block of 128 positions (128 b to 128 b + 127). In every aligned tile of 128 triple columns all tails lie in one aligned block of 128 positions.
All inputs are finite; a program needn't handle non-finite values.
Results may differ from a plain program's by a relative error of at most 0.0029.
Values sent between devices are 32-bit elements; how exact they have to be, the bound alone decides.
A program may use at most 128 MiB of HBM per device.

v0:
```python
import math

import jax
import jax.numpy as jnp
from jax import lax
from jax.sharding import PartitionSpec as P

ITERS = 8


ridge_weight = 0.01
tile_width = 128


def apply_normal(gram_matrix, stacked):
    left_side = jnp.einsum("ab,kbc->kac", gram_matrix, stacked, precision=lax.Precision.HIGHEST)
    return (
        jnp.einsum("kac,cd->kad", left_side, gram_matrix, precision=lax.Precision.HIGHEST)
        + ridge_weight * stacked
    )


def two_products(residual, image_map):
    return lax.psum(
        (jnp.sum(residual * residual), jnp.sum(residual * image_map)), ("ent", "blk", "rel")
    )


def select_rows(entity_ids, block_table):
    group_size, width = entity_ids.shape
    tile_count = width // tile_width
    block_count = block_table.shape[0]
    tiled_ids = entity_ids.reshape(group_size, tile_count, tile_width)
    block_of = tiled_ids[:, :, 0] // tile_width
    block_pick = (
        block_of[:, :, None] == jnp.arange(block_count, dtype=jnp.int32)[None, None, :]
    ).astype(jnp.bfloat16)
    chosen = jnp.einsum(
        "gtb,bcr->gtcr", block_pick, block_table, preferred_element_type=jnp.float32
    ).astype(jnp.bfloat16)
    inside = tiled_ids % tile_width
    slot_pick = (
        inside[:, :, :, None] == jnp.arange(tile_width, dtype=jnp.int32)[None, None, None, :]
    ).astype(jnp.bfloat16)
    return jnp.einsum("gtoc,gtcr->gtor", slot_pick, chosen, preferred_element_type=jnp.float32)


def body(factors, heads, tails, values):
    shards = lax.axis_size(("ent", "blk"))
    ent_dev = factors.shape[0]
    rank_width = factors.shape[1]
    triple_count = heads.shape[3]
    relation_rows = heads.shape[0] * heads.shape[2]
    norm_scale = 1.0 / math.sqrt(shards * triple_count)
    gram_total = lax.psum(
        jnp.dot(factors.T, factors, preferred_element_type=jnp.float32), ("ent", "blk")
    )
    gram_matrix = gram_total / (ent_dev * shards)
    block_table = factors.reshape(ent_dev // tile_width, tile_width, rank_width)
    head_ids = heads.reshape(relation_rows, triple_count)
    tail_ids = tails.reshape(relation_rows, triple_count)
    weights = values.reshape(relation_rows, triple_count)

    def grouped(operands):
        head_group, tail_group, weight_group = operands
        group_size = head_group.shape[0]
        tile_count = triple_count // tile_width
        head_rows = select_rows(head_group, block_table)
        weighted = (
            weight_group.reshape(group_size, tile_count, tile_width)[:, :, :, None] * head_rows
        ).astype(jnp.bfloat16)
        tail_rows = select_rows(tail_group, block_table).astype(jnp.bfloat16)
        product = jnp.einsum(
            "gtci,gtcj->gij", weighted, tail_rows, preferred_element_type=jnp.float32
        )
        return product * norm_scale

    own_rows = relation_rows // shards
    group_size = math.gcd(own_rows * lax.axis_size(("ent", "blk")), 4)
    group_total = own_rows * lax.axis_size(("ent", "blk")) // group_size
    shaped = (
        head_ids.reshape(group_total, group_size, triple_count),
        tail_ids.reshape(group_total, group_size, triple_count),
        weights.reshape(group_total, group_size, triple_count),
    )
    results = lax.map(grouped, shaped)
    target = lax.psum_scatter(
        results.reshape(own_rows * lax.axis_size(("ent", "blk")), rank_width, rank_width),
        ("ent", "blk"),
        scatter_dimension=0,
        tiled=True,
    )
    fitted = jnp.zeros_like(target)
    residual = target
    image_map = apply_normal(gram_matrix, residual)
    norm_now, product = two_products(residual, image_map)
    step_size = norm_now / product
    direction = residual
    along = image_map
    for step_index in range(ITERS):
        fitted = fitted + step_size * direction
        residual = residual - step_size * along
        if step_index + 1 < ITERS:
            image_map = apply_normal(gram_matrix, residual)
            norm_next, product = two_products(residual, image_map)
            ratio_next = norm_next / norm_now
            step_size = norm_next / (product - ratio_next * norm_next / step_size)
            direction = residual + ratio_next * direction
            along = image_map + ratio_next * along
            norm_now = norm_next
    return (fitted, residual)


def solution(mesh):
    placed = (
        P(("ent", "blk"), None),
        P(None, "rel", None, ("ent", "blk")),
        P(None, "rel", None, ("ent", "blk")),
        P(None, "rel", None, ("ent", "blk")),
    )
    return jax.shard_map(
        body,
        mesh=mesh,
        in_specs=placed,
        out_specs=(P(("ent", "blk", "rel"), None, None), P(("ent", "blk", "rel"), None, None)),
        check_vma=False,
    )
```

profile of v0, /device:TPU:0, one launch (start us, length us, event | category | flops | bytes accessed | tf_op | source)
XLA Modules:
  0.0 491.8 jit_solution(14854573454437355438)
XLA Ops:
  7.2 2.3 fusion.80
  11.7 17.5 %while.13 = (s32[]{:T(128)}, f32[2,4,256,256]{3,2,1,0:T(8,128)}, f32[2,4,1024]{2,1,0:T(4,128)S(1)}, s32[2,4,1024]{2,1,0:T(4,128)S(1)}, bf16[8,128,256]{2,0,1:T(8...) while((s32[]{:T(128)}, f32[2,4,256,256]{3,2,1,0:T(8,128)}, f32[2,4,1024]{2,1,0:T(4,128)S(1)}, ...), condition=%wide.region_1.2_spmd, body=%wide.region_0.0_spmd.sunk | while | flops 1113941504 | bytes 14992225 | solution.py:86
  12.7 2.7 multiply_convert_fusion.2
  16.4 4.1 fusion.113
  21.5 2.7 multiply_convert_fusion.2
  25.1 4.1 fusion.113
  29.3 39.0 %all-reduce.10.cloned.1.call-done = f32[256,256]{1,0:T(8,128)} async-done(((f32[256,256]{1,0:T(8,128)}), f32[256,256]{1,0:T(8,128)}) %all-reduce.10.cloned.1.call-update) | async-done | bytes 262160 | tf_op jit(solution)/shard_map/psum | solution.py:55
  68.3 43.8 %reduce-scatter.2.cloned.1.call-done = f32[1,256,256]{2,1,0:T(8,128)} async-done(((f32[8,256,256]{2,1,0:T(8,128)}), f32[1,256,256]{2,1,0:T(8,128)}) %reduce-scatter.2.cloned.1.call-update) | async-done | bytes 262160 | tf_op jit(solution)/shard_map/reduce_scatter | solution.py:87
  112.1 1.6 convolution_bitcast_fusion.15
  113.7 2.2 multiply_reduce_fusion.14
  116.0 39.5 %all-reduce.7 = (f32[]{:T(128)}, f32[]{:T(128)}) all-reduce(f32[]{:T(128)} %get-tuple-element.128, f32[]{:T(128)} %get-tuple-element.127), channel_id=1, replica_groups=mesh['ent'=2,'blk'=4,'rel'=4] {'ent','blk','rel'}, use_global_device_ids=true, to_apply=%region_4.5 | all-reduce | flops 2 | bytes 16 | tf_op jit(solution)/shard_map/psum | solution.py:24
  158.4 1.3 multiply_reduce_fusion.12
  159.7 41.4 %all-reduce.6 = (f32[]{:T(128)}, f32[]{:T(128)}) all-reduce(f32[]{:T(128)} %get-tuple-element.126, f32[]{:T(128)} %get-tuple-element.125), channel_id=1, replica_groups=mesh['ent'=2,'blk'=4,'rel'=4] {'ent','blk','rel'}, use_global_device_ids=true, to_apply=%region_9.10 | all-reduce | flops 2 | bytes 16 | tf_op jit(solution)/shard_map/psum | solution.py:24
  206.1 1.2 multiply_reduce_fusion.10
  207.3 39.6 %all-reduce.5 = (f32[]{:T(128)}, f32[]{:T(128)}) all-reduce(f32[]{:T(128)} %get-tuple-element.124, f32[]{:T(128)} %get-tuple-element.123), channel_id=1, replica_groups=mesh['ent'=2,'blk'=4,'rel'=4] {'ent','blk','rel'}, use_global_device_ids=true, to_apply=%region_13.14 | all-reduce | flops 2 | bytes 16 | tf_op jit(solution)/shard_map/psum | solution.py:24
  251.3 1.3 multiply_reduce_fusion.8
  252.6 41.5 %all-reduce.4 = (f32[]{:T(128)}, f32[]{:T(128)}) all-reduce(f32[]{:T(128)} %get-tuple-element.122, f32[]{:T(128)} %get-tuple-element.121), channel_id=1, replica_groups=mesh['ent'=2,'blk'=4,'rel'=4] {'ent','blk','rel'}, use_global_device_ids=true, to_apply=%region_17.18 | all-reduce | flops 2 | bytes 16 | tf_op jit(solution)/shard_map/psum | solution.py:24
  299.9 39.6 %all-reduce.3 = (f32[]{:T(128)}, f32[]{:T(128)}) all-reduce(f32[]{:T(128)} %get-tuple-element.120, f32[]{:T(128)} %get-tuple-element.119), channel_id=1, replica_groups=mesh['ent'=2,'blk'=4,'rel'=4] {'ent','blk','rel'}, use_global_device_ids=true, to_apply=%region_21.22 | all-reduce | flops 2 | bytes 16 | tf_op jit(solution)/shard_map/psum | solution.py:24
  344.1 1.3 multiply_reduce_fusion.4
  345.4 41.3 %all-reduce.2 = (f32[]{:T(128)}, f32[]{:T(128)}) all-reduce(f32[]{:T(128)} %get-tuple-element.118, f32[]{:T(128)} %get-tuple-element.117), channel_id=1, replica_groups=mesh['ent'=2,'blk'=4,'rel'=4] {'ent','blk','rel'}, use_global_device_ids=true, to_apply=%region_25.26 | all-reduce | flops 2 | bytes 16 | tf_op jit(solution)/shard_map/psum | solution.py:24
  391.3 1.2 multiply_reduce_fusion.2
  392.5 39.5 %all-reduce.1 = (f32[]{:T(128)}, f32[]{:T(128)}) all-reduce(f32[]{:T(128)} %get-tuple-element.116, f32[]{:T(128)} %get-tuple-element.115), channel_id=1, replica_groups=mesh['ent'=2,'blk'=4,'rel'=4] {'ent','blk','rel'}, use_global_device_ids=true, to_apply=%region_29.30 | all-reduce | flops 2 | bytes 16 | tf_op jit(solution)/shard_map/psum | solution.py:24
  436.7 1.3 multiply_reduce_fusion
  437.9 41.3 %all-reduce = (f32[]{:T(128)}, f32[]{:T(128)}) all-reduce(f32[]{:T(128)} %get-tuple-element.114, f32[]{:T(128)} %get-tuple-element.113), channel_id=1, replica_groups=mesh['ent'=2,'blk'=4,'rel'=4] {'ent','blk','rel'}, use_global_device_ids=true, to_apply=%region_33.34 | all-reduce | flops 2 | bytes 16 | tf_op jit(solution)/shard_map/psum | solution.py:24
  (59 shorter events, 14.3 us)
Async XLA Ops:
  7.2 4.2 copy-start.1
  7.2 4.5 copy-start.3
  7.2 61.1 %all-reduce.10.cloned.1.call-start = ((), (), s32[]{:S(2)}) async-start(), calls=%async_computation.2 | async-start | bytes 524288 | tf_op jit(solution)/shard_map/psum | solution.py:55
  9.5 102.6 %reduce-scatter.2.cloned.1.call-start = ((), (), s32[]{:S(2)}) async-start(), calls=%async_computation.1 | async-start | bytes 2359296 | tf_op jit(solution)/shard_map/reduce_scatter | solution.py:87
  68.3 89.5 %copy-start = (f32[256,256]{1,0:T(8,128)S(1)}, f32[256,256]{1,0:T(8,128)}, u32[]{:S(2)}) copy-start(f32[256,256]{1,0:T(8,128)} %all-reduce.10.cloned.1.call-done) | copy-start | bytes 786436
  436.0 48.0 %copy-start.2 = (f32[1,256,256]{2,1,0:T(8,128)S(1)}, f32[1,256,256]{2,1,0:T(8,128)}, u32[]{:S(2)}) copy-start(f32[1,256,256]{2,1,0:T(8,128)} %reduce-scatter.2.cloned.1.call-done) | copy-start | bytes 786436
Sparse Core Ops, SparseCore 0:
  11.6 56.6 all-reduce.9
  71.6 40.4 reduce-scatter.1
where the time goes:
time: 494 us; the launch traced here: 492 us
  blocking collectives  324 us (66%)
  waiting for transfers between devices  82.8 us (17%)
  between operations  43.5 us (9%)
  matrix products  35.6 us (7%)
  other arithmetic  5.49 us (1%)
    psum x8, blocking collectives, two_products(): lax.psum((jnp.sum(residual * residual), jnp.sum(residual * image_map)), (...  324 us
    reduce_scatter x1, waiting for transfers between devices, body(): lax.psum_scatter(results.reshape(own_rows * lax.axis_size(('ent', 'blk'))...  43.8 us
    psum x1, waiting for transfers between devices, body(): lax.psum(jnp.dot(factors.T, factors, preferred_element_type=jnp.float32),...  39 us
    dot_general x8, matrix products, apply_normal(): jnp.einsum('kac,cd->kad', left_side, gram_matrix, precision=lax.Precision...  10.9 us
  transfers between devices with their start and end apart: 2, of which 2 were waited for; matrix products, arithmetic and copies ran while one was open for 4% of the time, Pallas kernels for 0%

commit v1 on v0

--- a/solution.py
+++ b/solution.py
@@ -1,8 +1,11 @@
+import functools
 import math
 
 import jax
 import jax.numpy as jnp
 from jax import lax
+from jax.experimental import pallas as pl
+from jax.experimental.pallas import tpu as pltpu
 from jax.sharding import PartitionSpec as P
 
 ITERS = 8
@@ -111,6 +114,332 @@
     return (fitted, residual)
 
 
+MESH = pl.DeviceIdType.MESH
+COPIES = 32
+
+
+def fused_kernel(
+    z_count, scale_gram, scale_target,
+    factors_ref, heads_ref, tails_ref, values_ref, head_ids, tail_ids,
+    fit_ref, res_ref,
+    turned, left_rows, right_rows,
+    gram_part, gram_in, gram_half, gram_xy, gram_full, gram_pair,
+    pair_out, pair_in, own_sum, first_a, first_b, second_a, second_b,
+    basis, table, send_sem, recv_sem,
+):
+    f32, bf16 = jnp.float32, jnp.bfloat16
+    width = factors_ref.shape[1]
+    half = width // 2
+    quarter = width // 4
+    triples = heads_ref.shape[3]
+    e = lax.axis_index("ent")
+    b = lax.axis_index("blk")
+    z = lax.axis_index("rel")
+    y = b // 2
+    c = b % 2
+    pair_peer = (e, y * 2 + 1 - c, z)
+    x_peer = (1 - e, b, z)
+    y_peer = (e, (1 - y) * 2 + c, z)
+
+    def group_peer(mask):
+        me, my, mc = mask // 4, (mask // 2) % 2, mask % 2
+        return (
+            (1 - e) if me else e,
+            ((1 - y) if my else y) * 2 + ((1 - c) if mc else c),
+            z,
+        )
+
+    def z_peer(hop):
+        return (e, b, lax.rem(z + hop, z_count))
+
+    peers = [group_peer(m) for m in range(1, 8)] + [z_peer(h) for h in range(1, z_count)]
+    barrier = pltpu.get_barrier_semaphore()
+    for peer in peers:
+        pl.semaphore_signal(barrier, inc=1, device_id=peer, device_id_type=MESH)
+
+    counter = [0]
+
+    def send(source, dest, peer):
+        slot = counter[0]
+        counter[0] += 1
+        copy = pltpu.make_async_remote_copy(
+            src_ref=source, dst_ref=dest,
+            send_sem=send_sem.at[slot], recv_sem=recv_sem.at[slot],
+            device_id=peer, device_id_type=MESH,
+        )
+        copy.start()
+        return copy
+
+    flipped = factors_ref[...].T
+    for block in range(turned.shape[0]):
+        turned[block] = flipped[:, block * tile_width : (block + 1) * tile_width]
+    gram_part[...] = lax.dot_general(
+        flipped, flipped, (((1,), (1,)), ((), ())), preferred_element_type=f32
+    )
+    pl.semaphore_wait(barrier, len(peers))
+    own_rows = pl.ds(pl.multiple_of(c * half, half), half)
+    other_rows = pl.ds(pl.multiple_of((1 - c) * half, half), half)
+    g_pair = send(gram_part.at[other_rows], gram_in, pair_peer)
+
+    row_number = lax.broadcasted_iota(jnp.int32, (tile_width, tile_width), 0)
+    blank = jnp.zeros((tile_width, tile_width), bf16)
+
+    def gathered(ids_ref, scalar_ref, q, first):
+        picks, blocks = [], []
+        for tile in (first, first + 1):
+            start = tile * tile_width
+            inside = lax.rem(ids_ref[q, 0, :, start : start + tile_width], tile_width)
+            picks.append(jnp.where(row_number == inside, 1.0, 0.0).astype(bf16))
+            blocks.append(turned[lax.div(scalar_ref[q, 0, 0, start], tile_width)])
+        mixed = jnp.concatenate(
+            [
+                jnp.concatenate([picks[0], blank], axis=1),
+                jnp.concatenate([blank, picks[1]], axis=1),
+            ],
+            axis=0,
+        )
+        return jnp.dot(jnp.concatenate(blocks, axis=1), mixed, preferred_element_type=f32)
+
+    def partial(pe, py, pc):
+        q = pe * 4 + py * 2 + pc
+        for first in range(0, triples // tile_width, 2):
+            cols = slice(first * tile_width, (first + 2) * tile_width)
+            rows = gathered(heads_ref, head_ids, q, first)
+            left_rows[:, cols] = (values_ref[q, 0, :, cols] * rows).astype(bf16)
+            right_rows[:, cols] = gathered(tails_ref, tail_ids, q, first).astype(bf16)
+        return lax.dot_general(
+            left_rows[...], right_rows[...], (((1,), (1,)), ((), ())), preferred_element_type=f32
+        )
+
+    targets = ((1 - e, 1 - y), (1 - e, y), (e, 1 - y), (e, y))
+    pair_copies = []
+
+    def give(index):
+        pe, py = targets[index]
+        pair_out[index] = partial(pe, py, 1 - c)
+        pair_copies.append(send(pair_out.at[index], pair_in.at[index], pair_peer))
+
+    def keep(index):
+        pe, py = targets[index]
+        own_sum[index] = partial(pe, py, c)
+        pair_copies[index].wait()
+        own_sum[index] = own_sum[index] + pair_in[index]
+
+    top, low = pl.ds(0, half), pl.ds(half, half)
+    give(0)
+    g_pair.wait()
+    gram_half[0] = gram_part[own_rows, :] + gram_in[...]
+    g_a1 = send(gram_half.at[0, pl.ds(0, quarter)], gram_xy.at[0, pl.ds(0, quarter)], x_peer)
+    g_b1 = send(
+        gram_half.at[0, pl.ds(quarter, quarter)], gram_xy.at[0, pl.ds(quarter, quarter)], y_peer
+    )
+    keep(0)
+    a_diag = send(own_sum.at[0, top], first_a.at[0], x_peer)
+    b_diag = send(own_sum.at[0, low], first_b.at[0], y_peer)
+    give(1)
+    g_a1.wait()
+    g_b1.wait()
+    gram_half[1] = gram_half[0] + gram_xy[0]
+    g_a2 = send(gram_half.at[1, pl.ds(0, quarter)], gram_xy.at[1, pl.ds(0, quarter)], y_peer)
+    g_b2 = send(
+        gram_half.at[1, pl.ds(quarter, quarter)], gram_xy.at[1, pl.ds(quarter, quarter)], x_peer
+    )
+    keep(1)
+    a_side = send(own_sum.at[1, top], first_a.at[1], x_peer)
+    give(2)
+    keep(2)
+    b_side = send(own_sum.at[2, low], first_b.at[1], y_peer)
+    a_diag.wait()
+    second_a[0] = own_sum[2, :half, :] + first_a[0]
+    a_last = send(second_a.at[0], second_a.at[1], y_peer)
+    b_diag.wait()
+    second_b[0] = own_sum[1, half:, :] + first_b[0]
+    b_last = send(second_b.at[0], second_b.at[1], x_peer)
+    g_a2.wait()
+    g_b2.wait()
+    gram_pair[0] = gram_half[1] + gram_xy[1]
+    g_full = send(gram_pair.at[0], gram_pair.at[1], pair_peer)
+    give(3)
+    keep(3)
+    g_full.wait()
+    gram_full[own_rows, :] = gram_pair[0] * scale_gram
+    gram_full[other_rows, :] = gram_pair[1] * scale_gram
+    gram = gram_full[...]
+    gram_high = gram.astype(bf16)
+    gram_low = (gram - gram_high.astype(f32)).astype(bf16)
+    gram_both = jnp.concatenate([gram_high, gram_low], axis=0)
+    a_side.wait()
+    b_side.wait()
+    a_last.wait()
+    b_last.wait()
+    basis[0, :half, :] = ((own_sum[3, :half, :] + first_a[1]) + second_a[1]) * scale_target
+    basis[0, half:, :] = ((own_sum[3, half:, :] + first_b[1]) + second_b[1]) * scale_target
+
+    def split(value):
+        high = value.astype(bf16)
+        return high, (value - high.astype(f32)).astype(bf16)
+
+    def total(value):
+        return jnp.sum(jnp.sum(value, axis=0, keepdims=True), axis=1, keepdims=True)
+
+    def normal_map(value):
+        high, low_part = split(value)
+        both = jnp.dot(gram_both, high, preferred_element_type=f32)
+        inner = both[:width] + (
+            both[width:] + jnp.dot(gram_high, low_part, preferred_element_type=f32)
+        )
+        high, low_part = split(inner)
+        both = jnp.dot(
+            jnp.concatenate([high, low_part], axis=0), gram_high, preferred_element_type=f32
+        )
+        outer = both[:width] + (
+            both[width:] + jnp.dot(high, gram_low, preferred_element_type=f32)
+        )
+        return outer + ridge_weight * value
+
+    lane = lax.broadcasted_iota(jnp.int32, (1, 128), 1)
+    record = jnp.zeros((1, 128), f32)
+    inverses = []
+    for index in range(ITERS):
+        vector = basis[index]
+        image = normal_map(vector)
+        square = total(vector * vector)
+        cross = total(vector * image)
+        inverse = jnp.where(square > 0.0, lax.rsqrt(square), 0.0)
+        length = square * inverse
+        diagonal = (cross * inverse) * inverse
+        record = jnp.where(lane == index, diagonal, record)
+        record = jnp.where(lane == ITERS + index, length, record)
+        if index + 1 == ITERS:
+            table[0, 0] = record
+            z_copies = [
+                send(table.at[0, 0], table.at[0, z_count - hop], z_peer(hop))
+                for hop in range(1, z_count)
+            ]
+        following = (image - diagonal * vector) * inverse
+        if index > 0:
+            following = following - (length * inverses[-1]) * basis[index - 1]
+        inverses.append(inverse)
+        basis[index + 1] = following
+    for copy in z_copies:
+        copy.wait()
+    group_copies = [send(table.at[0], table.at[m], group_peer(m)) for m in range(1, 8)]
+    for copy in group_copies:
+        copy.wait()
+
+    lines = table[...].reshape(8 * z_count, 128)
+    filled = jnp.concatenate([lines, jnp.zeros((128 - 8 * z_count, 128), f32)], axis=0).T
+    alpha = [filled[j : j + 1, :] for j in range(ITERS)]
+    beta = [filled[ITERS + j : ITERS + j + 1, :] for j in range(ITERS)] + [
+        jnp.ones((1, 128), f32)
+    ]
+
+    def reduced(rows):
+        added = rows[0]
+        for row in rows[1:]:
+            added = added + row
+        return jnp.sum(added, axis=1, keepdims=True)
+
+    def small_map(rows):
+        count = len(rows)
+        made = []
+        for j in range(count + 1):
+            entry = None
+            if j < count:
+                entry = alpha[j] * rows[j]
+            if j > 0:
+                term = beta[j] * rows[j - 1]
+                entry = term if entry is None else entry + term
+            if j + 1 < count:
+                entry = entry + beta[j + 1] * rows[j + 1]
+            made.append(entry)
+        return made
+
+    def mixed_sum(first, ratio, second):
+        return [
+            one + ratio * second[j] if j < len(second) else one for j, one in enumerate(first)
+        ]
+
+    residual = [beta[0]]
+    image = small_map(residual)
+    norm_now = reduced([row * row for row in residual])
+    product = reduced([row * image[j] for j, row in enumerate(residual)])
+    step_size = norm_now / product
+    direction, along = residual, image
+    fitted = []
+    for index in range(ITERS):
+        fitted = [
+            fitted[j] + step_size * row if j < len(fitted) else step_size * row
+            for j, row in enumerate(direction)
+        ]
+        residual = [
+            residual[j] - step_size * row if j < len(residual) else -(step_size * row)
+            for j, row in enumerate(along)
+        ]
+        if index + 1 < ITERS:
+            image = small_map(residual)
+            norm_next = reduced([row * row for row in residual])
+            product = reduced([row * image[j] for j, row in enumerate(residual)])
+            ratio = norm_next / norm_now
+            step_size = norm_next / (product - ratio * norm_next / step_size)
+            direction = mixed_sum(residual, ratio, direction)
+            along = mixed_sum(image, ratio, along)
+            norm_now = norm_next
+    inverses.append(jnp.ones((1, 1), f32))
+    fit_weights = [row[:, 0:1] * inverses[j] for j, row in enumerate(fitted)]
+    res_weights = [row[:, 0:1] * inverses[j] for j, row in enumerate(residual)]
+    fit = fit_weights[0] * basis[0]
+    res = res_weights[0] * basis[0]
+    for j in range(1, ITERS):
+        fit = fit + fit_weights[j] * basis[j]
+        res = res + res_weights[j] * basis[j]
+    fit_ref[0] = fit
+    res_ref[0] = res + res_weights[ITERS] * basis[ITERS]
+
+
+def fused_body(factors, heads, tails, values):
+    shards = lax.axis_size(("ent", "blk"))
+    z_count = lax.axis_size("rel")
+    ent_dev, width = factors.shape
+    triples = heads.shape[3]
+    half = width // 2
+    f32, bf16 = jnp.float32, jnp.bfloat16
+    vmem = pl.BlockSpec(memory_space=pltpu.VMEM)
+    smem = pl.BlockSpec(memory_space=pltpu.SMEM)
+    out = jax.ShapeDtypeStruct((1, width, width), f32)
+    return pl.pallas_call(
+        functools.partial(
+            fused_kernel, z_count, 1.0 / (ent_dev * shards), 1.0 / math.sqrt(shards * triples)
+        ),
+        out_shape=(out, out),
+        in_specs=[vmem] * 4 + [smem] * 2,
+        out_specs=(vmem, vmem),
+        scratch_shapes=[
+            pltpu.VMEM((ent_dev // tile_width, width, tile_width), bf16),
+            pltpu.VMEM((width, triples), bf16),
+            pltpu.VMEM((width, triples), bf16),
+            pltpu.VMEM((width, width), f32),
+            pltpu.VMEM((half, width), f32),
+            pltpu.VMEM((2, half, width), f32),
+            pltpu.VMEM((2, half, width), f32),
+            pltpu.VMEM((width, width), f32),
+            pltpu.VMEM((2, half, width), f32),
+            pltpu.VMEM((4, width, width), f32),
+            pltpu.VMEM((4, width, width), f32),
+            pltpu.VMEM((4, width, width), f32),
+            pltpu.VMEM((2, half, width), f32),
+            pltpu.VMEM((2, half, width), f32),
+            pltpu.VMEM((2, half, width), f32),
+            pltpu.VMEM((2, half, width), f32),
+            pltpu.VMEM((ITERS + 1, width, width), f32),
+            pltpu.VMEM((8, z_count, 1, 128), f32),
+            pltpu.SemaphoreType.DMA((COPIES,)),
+            pltpu.SemaphoreType.DMA((COPIES,)),
+        ],
+        compiler_params=pltpu.CompilerParams(collective_id=0, has_side_effects=True),
+    )(factors, heads, tails, values, heads, tails)
+
+
 def solution(mesh):
     placed = (
         P(("ent", "blk"), None),
@@ -118,8 +447,10 @@
         P(None, "rel", None, ("ent", "blk")),
         P(None, "rel", None, ("ent", "blk")),
     )
+    sizes = dict(mesh.shape)
+    fused = sizes["ent"] == 2 and sizes["blk"] == 4 and 1 < sizes["rel"] <= 16
     return jax.shard_map(
-        body,
+        fused_body if fused else body,
         mesh=mesh,
         in_specs=placed,
         out_specs=(P(("ent", "blk", "rel"), None, None), P(("ent", "blk", "rel"), None, None)),

time: 494 us -> 41.5 us (0.08)
  blocking collectives: 324 us -> 0 us
  waiting for transfers between devices: 82.8 us -> 0 us
  between operations: 43.5 us -> 0.65 us
  Pallas kernels: 0 us -> 38.2 us
  matrix products: 35.6 us -> 0 us
  other arithmetic: 5.49 us -> 0 us
    psum x8 -> x0, blocking collectives: 324 us -> none  [two_products(): lax.psum((jnp.sum(residual * residual), jnp.sum(residual * image_map)), (...]
    reduce_scatter x1 -> x0, waiting for transfers between devices: 43.8 us -> none  [body(): lax.psum_scatter(results.reshape(own_rows * lax.axis_size(('ent', 'blk'))...]
    psum x1 -> x0, waiting for transfers between devices: 39 us -> none  [body(): lax.psum(jnp.dot(factors.T, factors, preferred_element_type=jnp.float32),...]
    pallas_call x0 -> x1, Pallas kernels: none -> 38.2 us  [fused_body(): pl.pallas_call(functools.partial(fused_kernel, z_count, 1.0 / (ent_dev *...]
    dot_general x25 -> x0, matrix products: 35.6 us -> none  [the longest x8 10.9 us: apply_normal(): jnp.einsum('kac,cd->kad', left_side, gram_matrix, precision=lax.Precision...]
  transfers between devices with their start and end apart: 2 -> 0, of which waited for: 2 -> 0; matrix products, arithmetic and copies ran while one was open for 4% -> 0% of each run, Pallas kernels for 0% -> 0%
where the time goes in v1:
time: 41.5 us; the launch traced here: 41.3 us
  Pallas kernels  38.2 us (92%)
  local copies, waits for them, and re-layouts  2.42 us (6%)
  between operations  0.65 us (2%)
    pallas_call x1, Pallas kernels, fused_body(): pl.pallas_call(functools.partial(fused_kernel, z_count, 1.0 / (ent_dev *...  38.2 us
    unnamed x4, local copies, waits for them, and re-layouts  2.42 us

profile of v1, /device:TPU:0, one launch (start us, length us, event | category | flops | bytes accessed | tf_op | source)
XLA Modules:
  0.0 41.3 jit_solution(8232373660018638919)
XLA Ops:
  0.6 38.2 %shard_map.59 = (f32[1,256,256]{2,1,0:T(8,128)}, f32[1,256,256]{2,1,0:T(8,128)}) custom-call(bf16[1024,256]{1,0:T(8,128)(2,1)} %factors_ref.1, s32[8,1,1,1024]{3,2,1,0:T(1,128)} %head_ids.1, s32[8,1,1,1024]{3,2,1,0:T(1,128)} %tail_ids.1, f32[8,1,1,1024]{3,2,1,0:T(1,128)} %values_ref.1, s32[8,1,1,1024]{3,2,1,0:T(1,128)} %head_ids.1, s32[8,1,1,1024]{3,2,1,0:T(1,128)} %tail_ids.1), custom_call_target="tpu_custom_call" | custom-call | tf_op jit(solution)/shard_map/pallas_call | solution.py:410
  38.9 0.0 copy-start
  38.9 1.7 %copy.8 = f32[1,256,256]{2,1,0:T(8,128)} copy(f32[1,256,256]{2,1,0:T(8,128)} %get-tuple-element.4) | data formatting | bytes 524288
  40.6 0.0 copy-done
  40.6 0.7 %copy.9 = f32[1,256,256]{2,1,0:T(8,128)} copy(f32[1,256,256]{2,1,0:T(8,128)S(1)} %copy-done) | data formatting | bytes 524288
Async XLA Ops:
  38.9 1.7 %copy-start = (f32[1,256,256]{2,1,0:T(8,128)S(1)}, f32[1,256,256]{2,1,0:T(8,128)}, u32[]{:S(2)}) copy-start(f32[1,256,256]{2,1,0:T(8,128)} %get-tuple-element.5) | copy-start | bytes 786436

commit v2 on v1

--- a/solution.py
+++ b/solution.py
@@ -120,17 +120,19 @@
 
 def fused_kernel(
     z_count, scale_gram, scale_target,
-    factors_ref, heads_ref, tails_ref, values_ref, head_ids, tail_ids,
+    factors_hbm, heads_hbm, tails_hbm, values_hbm,
     fit_ref, res_ref,
+    factors_ref, heads_ref, tails_ref, values_ref, head_ids, tail_ids, load_sem, ready,
     turned, left_rows, right_rows,
-    gram_part, gram_in, gram_half, gram_xy, gram_full, gram_pair,
+    gram_part, gram_in, gram_half, gram_xy, gram_line, gram_full, gram_pair,
     pair_out, pair_in, own_sum, first_a, first_b, second_a, second_b,
     basis, table, send_sem, recv_sem,
 ):
     f32, bf16 = jnp.float32, jnp.bfloat16
     width = factors_ref.shape[1]
     half = width // 2
-    quarter = width // 4
+    share = half // z_count
+    part = share // 2
     triples = heads_ref.shape[3]
     e = lax.axis_index("ent")
     b = lax.axis_index("blk")
@@ -152,10 +154,35 @@
     def z_peer(hop):
         return (e, b, lax.rem(z + hop, z_count))
 
-    peers = [group_peer(m) for m in range(1, 8)] + [z_peer(h) for h in range(1, z_count)]
+    near = [group_peer(m) for m in (1, 2, 4)]
+    inner = ((z > 0, -1), (z < z_count - 1, 1))
+
+    def tell(semaphore):
+        for present, hop in inner:
+            @pl.when(present)
+            def _():
+                pl.semaphore_signal(
+                    semaphore, inc=1, device_id=(e, b, z + hop), device_id_type=MESH
+                )
+
+    line_count = jnp.where(z > 0, 1, 0) + jnp.where(z < z_count - 1, 1, 0)
     barrier = pltpu.get_barrier_semaphore()
-    for peer in peers:
+    for peer in near:
         pl.semaphore_signal(barrier, inc=1, device_id=peer, device_id_type=MESH)
+    tell(barrier)
+    loads = []
+    for slot, (source, dest) in enumerate(
+        (
+            (factors_hbm, factors_ref),
+            (heads_hbm, head_ids),
+            (tails_hbm, tail_ids),
+            (heads_hbm, heads_ref),
+            (values_hbm, values_ref),
+            (tails_hbm, tails_ref),
+        )
+    ):
+        loads.append(pltpu.make_async_copy(source, dest, load_sem.at[slot]))
+        loads[-1].start()
 
     counter = [0]
 
@@ -170,16 +197,17 @@
         copy.start()
         return copy
 
+    loads[0].wait()
     flipped = factors_ref[...].T
     for block in range(turned.shape[0]):
         turned[block] = flipped[:, block * tile_width : (block + 1) * tile_width]
     gram_part[...] = lax.dot_general(
         flipped, flipped, (((1,), (1,)), ((), ())), preferred_element_type=f32
     )
-    pl.semaphore_wait(barrier, len(peers))
     own_rows = pl.ds(pl.multiple_of(c * half, half), half)
     other_rows = pl.ds(pl.multiple_of((1 - c) * half, half), half)
-    g_pair = send(gram_part.at[other_rows], gram_in, pair_peer)
+    own_share = pl.ds(pl.multiple_of(c * half + z * share, share), share)
+    other_share = pl.ds(pl.multiple_of((1 - c) * half + z * share, share), share)
 
     row_number = lax.broadcasted_iota(jnp.int32, (tile_width, tile_width), 0)
     blank = jnp.zeros((tile_width, tile_width), bf16)
@@ -226,13 +254,21 @@
         own_sum[index] = own_sum[index] + pair_in[index]
 
     top, low = pl.ds(0, half), pl.ds(half, half)
-    give(0)
+    for load in loads[1:]:
+        load.wait()
+    pair_out[0] = partial(1 - e, 1 - y, 1 - c)
+    pl.semaphore_wait(barrier, len(near) + line_count)
+    g_pair = send(gram_part.at[other_share], gram_in, pair_peer)
+    pair_copies.append(send(pair_out.at[0], pair_in.at[0], pair_peer))
+    for step in range(z_count - 2):
+        tell(ready.at[step])
+        if step + 1 < z_count - 2:
+            pl.semaphore_wait(ready.at[step], line_count)
     g_pair.wait()
-    gram_half[0] = gram_part[own_rows, :] + gram_in[...]
-    g_a1 = send(gram_half.at[0, pl.ds(0, quarter)], gram_xy.at[0, pl.ds(0, quarter)], x_peer)
-    g_b1 = send(
-        gram_half.at[0, pl.ds(quarter, quarter)], gram_xy.at[0, pl.ds(quarter, quarter)], y_peer
-    )
+    gram_half[0] = gram_part[own_share, :] + gram_in[...]
+    upper, lower = pl.ds(0, part), pl.ds(part, part)
+    g_a1 = send(gram_half.at[0, upper], gram_xy.at[0, upper], x_peer)
+    g_b1 = send(gram_half.at[0, lower], gram_xy.at[0, lower], y_peer)
     keep(0)
     a_diag = send(own_sum.at[0, top], first_a.at[0], x_peer)
     b_diag = send(own_sum.at[0, low], first_b.at[0], y_peer)
@@ -240,13 +276,20 @@
     g_a1.wait()
     g_b1.wait()
     gram_half[1] = gram_half[0] + gram_xy[0]
-    g_a2 = send(gram_half.at[1, pl.ds(0, quarter)], gram_xy.at[1, pl.ds(0, quarter)], y_peer)
-    g_b2 = send(
-        gram_half.at[1, pl.ds(quarter, quarter)], gram_xy.at[1, pl.ds(quarter, quarter)], x_peer
-    )
+    g_a2 = send(gram_half.at[1, upper], gram_xy.at[1, upper], y_peer)
+    g_b2 = send(gram_half.at[1, lower], gram_xy.at[1, lower], x_peer)
     keep(1)
     a_side = send(own_sum.at[1, top], first_a.at[1], x_peer)
     give(2)
+    g_a2.wait()
+    g_b2.wait()
+    gram_line[0] = gram_half[1] + gram_xy[1]
+    if z_count > 2:
+        pl.semaphore_wait(ready.at[z_count - 3], line_count)
+    line_copies = [
+        send(gram_line.at[0], gram_line.at[z_count - hop], z_peer(hop))
+        for hop in range(1, z_count)
+    ]
     keep(2)
     b_side = send(own_sum.at[2, low], first_b.at[1], y_peer)
     a_diag.wait()
@@ -255,9 +298,11 @@
     b_diag.wait()
     second_b[0] = own_sum[1, half:, :] + first_b[0]
     b_last = send(second_b.at[0], second_b.at[1], x_peer)
-    g_a2.wait()
-    g_b2.wait()
-    gram_pair[0] = gram_half[1] + gram_xy[1]
+    for copy in line_copies:
+        copy.wait()
+    for hop in range(z_count):
+        place = lax.rem(z + hop, z_count)
+        gram_pair[0, pl.ds(pl.multiple_of(place * share, share), share), :] = gram_line[hop]
     g_full = send(gram_pair.at[0], gram_pair.at[1], pair_peer)
     give(3)
     keep(3)
@@ -405,23 +450,32 @@
     half = width // 2
     f32, bf16 = jnp.float32, jnp.bfloat16
     vmem = pl.BlockSpec(memory_space=pltpu.VMEM)
-    smem = pl.BlockSpec(memory_space=pltpu.SMEM)
-    out = jax.ShapeDtypeStruct((1, width, width), f32)
+    out = pltpu.VMEM((1, width, width), f32)
+    share = half // z_count
     return pl.pallas_call(
         functools.partial(
             fused_kernel, z_count, 1.0 / (ent_dev * shards), 1.0 / math.sqrt(shards * triples)
         ),
         out_shape=(out, out),
-        in_specs=[vmem] * 4 + [smem] * 2,
+        in_specs=[pl.BlockSpec(memory_space=pl.ANY)] * 4,
         out_specs=(vmem, vmem),
         scratch_shapes=[
+            pltpu.VMEM(factors.shape, bf16),
+            pltpu.VMEM(heads.shape, jnp.int32),
+            pltpu.VMEM(tails.shape, jnp.int32),
+            pltpu.VMEM(values.shape, f32),
+            pltpu.SMEM(heads.shape, jnp.int32),
+            pltpu.SMEM(tails.shape, jnp.int32),
+            pltpu.SemaphoreType.DMA((6,)),
+            pltpu.SemaphoreType.REGULAR((max(z_count - 2, 1),)),
             pltpu.VMEM((ent_dev // tile_width, width, tile_width), bf16),
             pltpu.VMEM((width, triples), bf16),
             pltpu.VMEM((width, triples), bf16),
             pltpu.VMEM((width, width), f32),
-            pltpu.VMEM((half, width), f32),
-            pltpu.VMEM((2, half, width), f32),
-            pltpu.VMEM((2, half, width), f32),
+            pltpu.VMEM((share, width), f32),
+            pltpu.VMEM((2, share, width), f32),
+            pltpu.VMEM((2, share, width), f32),
+            pltpu.VMEM((z_count, share, width), f32),
             pltpu.VMEM((width, width), f32),
             pltpu.VMEM((2, half, width), f32),
             pltpu.VMEM((4, width, width), f32),
@@ -437,7 +491,7 @@
             pltpu.SemaphoreType.DMA((COPIES,)),
         ],
         compiler_params=pltpu.CompilerParams(collective_id=0, has_side_effects=True),
-    )(factors, heads, tails, values, heads, tails)
+    )(factors, heads, tails, values)
 
 
 def solution(mesh):
@@ -448,7 +502,7 @@
         P(None, "rel", None, ("ent", "blk")),
     )
     sizes = dict(mesh.shape)
-    fused = sizes["ent"] == 2 and sizes["blk"] == 4 and 1 < sizes["rel"] <= 16
+    fused = sizes["ent"] == 2 and sizes["blk"] == 4 and sizes["rel"] in (2, 4, 8)
     return jax.shard_map(
         fused_body if fused else body,
         mesh=mesh,

time: 41.5 us -> 38.8 us (0.935)
  Pallas kernels: 38.2 us -> 36.5 us
  local copies, waits for them, and re-layouts: 2.42 us -> 1.41 us
    pallas_call x1, Pallas kernels: 38.2 us -> 36.5 us  [fused_body(): pl.pallas_call(functools.partial(fused_kernel, z_count, 1.0 / (ent_dev *...]
    unnamed x4 -> x2, local copies, waits for them, and re-layouts: 2.42 us -> 1.41 us
where the time goes in v2:
time: 38.8 us; the launch traced here: 38.6 us
  Pallas kernels  36.5 us (94%)
  local copies, waits for them, and re-layouts  1.41 us (4%)
  between operations  0.64 us (2%)
    pallas_call x1, Pallas kernels, fused_body(): pl.pallas_call(functools.partial(fused_kernel, z_count, 1.0 / (ent_dev *...  36.5 us
    unnamed x2, local copies, waits for them, and re-layouts  1.41 us

profile of v2, /device:TPU:0, one launch (start us, length us, event | category | flops | bytes accessed | tf_op | source)
XLA Modules:
  0.0 38.6 jit_solution(15671735348491912907)
XLA Ops:
  0.6 36.5 %shard_map.59 = (f32[1,256,256]{2,1,0:T(8,128)S(1)}, f32[1,256,256]{2,1,0:T(8,128)S(1)}) custom-call(bf16[1024,256]{1,0:T(8,128)(2,1)} %factors_hbm.1, s32[8,1,1,1024]{3,2,1,0:T(1,128)} %heads_hbm.1, s32[8,1,1,1024]{3,2,1,0:T(1,128)} %tails_hbm.1, f32[8,1,1,1024]{3,2,1,0:T(1,128)} %values_hbm.1), custom_call_target="tpu_custom_call" | custom-call | tf_op jit(solution)/shard_map/pallas_call | solution.py:455
  37.2 0.7 %copy.8 = f32[1,256,256]{2,1,0:T(8,128)} copy(f32[1,256,256]{2,1,0:T(8,128)S(1)} %get-tuple-element.2) | data formatting | bytes 524288
  37.9 0.7 %copy.9 = f32[1,256,256]{2,1,0:T(8,128)} copy(f32[1,256,256]{2,1,0:T(8,128)S(1)} %get-tuple-element.3) | data formatting | bytes 524288

commit v3 on v2

--- a/solution.py
+++ b/solution.py
@@ -115,7 +115,7 @@
 
 
 MESH = pl.DeviceIdType.MESH
-COPIES = 32
+COPIES = 64
 
 
 def fused_kernel(
@@ -298,14 +298,14 @@
     b_diag.wait()
     second_b[0] = own_sum[1, half:, :] + first_b[0]
     b_last = send(second_b.at[0], second_b.at[1], x_peer)
+    give(3)
+    keep(3)
     for copy in line_copies:
         copy.wait()
     for hop in range(z_count):
         place = lax.rem(z + hop, z_count)
         gram_pair[0, pl.ds(pl.multiple_of(place * share, share), share), :] = gram_line[hop]
     g_full = send(gram_pair.at[0], gram_pair.at[1], pair_peer)
-    give(3)
-    keep(3)
     g_full.wait()
     gram_full[own_rows, :] = gram_pair[0] * scale_gram
     gram_full[other_rows, :] = gram_pair[1] * scale_gram
@@ -357,19 +357,22 @@
         record = jnp.where(lane == ITERS + index, length, record)
         if index + 1 == ITERS:
             table[0, 0] = record
-            z_copies = [
-                send(table.at[0, 0], table.at[0, z_count - hop], z_peer(hop))
-                for hop in range(1, z_count)
+            far_copies = [
+                send(
+                    table.at[0, 0],
+                    table.at[m, (z_count - hop) % z_count],
+                    group_peer(m)[:2] + (lax.rem(z + hop, z_count),),
+                )
+                for hop in range(z_count)
+                for m in range(8)
+                if m or hop
             ]
         following = (image - diagonal * vector) * inverse
         if index > 0:
             following = following - (length * inverses[-1]) * basis[index - 1]
         inverses.append(inverse)
         basis[index + 1] = following
-    for copy in z_copies:
-        copy.wait()
-    group_copies = [send(table.at[0], table.at[m], group_peer(m)) for m in range(1, 8)]
-    for copy in group_copies:
+    for copy in far_copies:
         copy.wait()
 
     lines = table[...].reshape(8 * z_count, 128)

time: 38.8 us -> 37.3 us (0.961)
  Pallas kernels: 36.5 us -> 35.1 us
    pallas_call x1, Pallas kernels: 36.5 us -> 35.1 us  [fused_body(): pl.pallas_call(functools.partial(fused_kernel, z_count, 1.0 / (ent_dev *...]
where the time goes in v3:
time: 37.3 us; the launch traced here: 37.1 us
  Pallas kernels  35.1 us (94%)
  local copies, waits for them, and re-layouts  1.41 us (4%)
  between operations  0.64 us (2%)
    pallas_call x1, Pallas kernels, fused_body(): pl.pallas_call(functools.partial(fused_kernel, z_count, 1.0 / (ent_dev *...  35.1 us
    unnamed x2, local copies, waits for them, and re-layouts  1.41 us

profile of v3, /device:TPU:0, one launch (start us, length us, event | category | flops | bytes accessed | tf_op | source)
XLA Modules:
  0.0 37.1 jit_solution(11279253009447900689)
XLA Ops:
  0.6 35.1 %shard_map.59 = (f32[1,256,256]{2,1,0:T(8,128)S(1)}, f32[1,256,256]{2,1,0:T(8,128)S(1)}) custom-call(bf16[1024,256]{1,0:T(8,128)(2,1)} %factors_hbm.1, s32[8,1,1,1024]{3,2,1,0:T(1,128)} %heads_hbm.1, s32[8,1,1,1024]{3,2,1,0:T(1,128)} %tails_hbm.1, f32[8,1,1,1024]{3,2,1,0:T(1,128)} %values_hbm.1), custom_call_target="tpu_custom_call" | custom-call | tf_op jit(solution)/shard_map/pallas_call | solution.py:458
  35.7 0.7 %copy.8 = f32[1,256,256]{2,1,0:T(8,128)} copy(f32[1,256,256]{2,1,0:T(8,128)S(1)} %get-tuple-element.2) | data formatting | bytes 524288
  36.4 0.7 %copy.9 = f32[1,256,256]{2,1,0:T(8,128)} copy(f32[1,256,256]{2,1,0:T(8,128)S(1)} %get-tuple-element.3) | data formatting | bytes 524288
